TPU v7x, 32 devices: a whole 2x2x4 slice. The times are simulated.
32 devices in a mesh: dp: 8 (over z, x), fsdp: 4 (over y, core).
Axes of the slice: x: 2, y: 2, z: 4, core: 2. Of those that a mesh axis runs over, the one named last changes fastest.
Arguments:
- tokens: bfloat16 [16384, 1024], P(('dp', 'fsdp')), may hold values from -6 to 6
- cluster_lengths: int32 [32, 8], P(('dp', 'fsdp')), may hold values from 1 to 128, 512 in all within a row
- norm_gain: bfloat16 [1024], P('fsdp'), may hold values from 0.099609375 to 1.8984375
- in_weight: bfloat16 [1024, 4096], P('fsdp'), may hold values from -0.1875 to 0.1875
- conv_weight: bfloat16 [4, 2048], P(None, 'fsdp'), may hold values from -3 to 3
- conv_bias: bfloat16 [2048], P('fsdp'), may hold values from -3 to 3
- xproj_weight: bfloat16 [2048, 96], P('fsdp'), may hold values from -0.125 to 0.125
- dt_weight: bfloat16 [64, 2048], P(None, 'fsdp'), may hold values from -0.75 to 0.75
- dt_bias: bfloat16 [2048], P('fsdp'), may hold values from -6.5 to -2
- a_log: bfloat16 [16, 2048], P(None, 'fsdp'), may hold values from 0 to 2.796875
- skip_gain: bfloat16 [2048], P('fsdp'), may hold values from 0.5 to 1.5
- out_weight: bfloat16 [2048, 1024], P('fsdp'), may hold values from -0.375 to 0.375
- cotangent: bfloat16 [16384, 1024], P(('dp', 'fsdp')), may hold values from -6 to 6
Outputs:
- output: bfloat16 [16384, 1024], P(('dp', 'fsdp'))
- input_grad: float32 [16384, 1024], P(('dp', 'fsdp'))
- gain_grad: float32 [1024], P('fsdp')
- in_grad: float32 [1024, 4096], P('fsdp')
- conv_weight_grad: float32 [4, 2048], P(None, 'fsdp')
- conv_bias_grad: float32 [2048], P('fsdp')
- xproj_grad: float32 [2048, 96], P('fsdp')
- dt_weight_grad: float32 [64, 2048], P(None, 'fsdp')
- dt_bias_grad: float32 [2048], P('fsdp')
- a_log_grad: float32 [16, 2048], P(None, 'fsdp')
- skip_grad: float32 [2048], P('fsdp')
- out_grad: float32 [2048, 1024], P('fsdp')
Inputs may be any that keep to these rules, and one draw needn't show every extreme that they name: `cluster_lengths`: each row holds the lengths of the 8 clusters packed into one context, in order; they sum to 512 and the longest is exactly 128.
All inputs are finite; a program needn't handle non-finite values.
Results may differ from a plain program's by a relative error of at most 0.011.
Values may be sent and summed in bfloat16 or wider, within the bound.
A program may use at most 256 MiB of HBM per device.

v0:
```python
import jax
import jax.numpy as jnp
from jax import lax
from jax.sharding import PartitionSpec as P

KCONV = 4
LENGTH = 512
BLOCK = 16


epsilon = 1e-05


def matmul(former, latter):
    return jnp.dot(former, latter, preferred_element_type=jnp.float32)


def left_inner(former, latter):
    return lax.dot_general(
        former, latter, (((0,), (0,)), ((), ())), preferred_element_type=jnp.float32
    )


def right_inner(former, latter):
    return lax.dot_general(
        former, latter, (((1,), (1,)), ((), ())), preferred_element_type=jnp.float32
    )


def silu_of(values):
    return values * jax.nn.sigmoid(values)


def silu_slope(values):
    logistic = jax.nn.sigmoid(values)
    return logistic * (1.0 + values * (1.0 - logistic))


def cluster_masks(lengths):
    cluster_ends = jnp.cumsum(lengths, axis=-1)
    starts = cluster_ends - lengths
    positions = jnp.arange(LENGTH, dtype=jnp.int32)
    before = starts[:, None, :] <= positions[None, :, None]
    segment_start = jnp.max(jnp.where(before, starts[:, None, :], 0), axis=-1)
    keep_mask = (positions[None, :] > segment_start).astype(jnp.float32)
    lag_index = jnp.arange(KCONV, dtype=jnp.int32)
    tap_valid = (
        positions[None, :, None] - lag_index[None, None, :] >= segment_start[:, :, None]
    ).astype(jnp.float32)
    return (tap_valid[0], keep_mask[0])


def to_blocks(values):
    row_count = values.shape[0]
    shaped = values.reshape((row_count // BLOCK, BLOCK) + values.shape[1:])
    return jnp.moveaxis(shaped, 1, 0)


def from_blocks(values):
    shaped = jnp.moveaxis(values, 0, 1)
    return shaped.reshape((-1,) + shaped.shape[2:])


def decay_factor(step_t, keep_t, decay_rate):
    return keep_t[:, None, None] * jnp.exp(step_t[:, None, :] * decay_rate[None])


def chained(earlier, later_item):
    return (earlier[0] * later_item[0], later_item[0] * earlier[1] + later_item[1])


def body(
    tokens,
    cluster_lengths,
    norm_gain,
    in_weight,
    conv_weight,
    conv_bias,
    xproj_weight,
    dt_weight,
    dt_bias,
    a_log,
    skip_gain,
    out_weight,
    cotangent,
):
    gathered = (
        lax.all_gather(norm_gain, "fsdp", axis=0, tiled=True),
        lax.all_gather(in_weight, "fsdp", axis=0, tiled=True),
        lax.all_gather(conv_weight, "fsdp", axis=1, tiled=True),
        lax.all_gather(conv_bias, "fsdp", axis=0, tiled=True),
        lax.all_gather(xproj_weight, "fsdp", axis=0, tiled=True),
        lax.all_gather(dt_weight, "fsdp", axis=1, tiled=True),
        lax.all_gather(dt_bias, "fsdp", axis=0, tiled=True),
        lax.all_gather(a_log, "fsdp", axis=1, tiled=True),
        lax.all_gather(skip_gain, "fsdp", axis=0, tiled=True),
        lax.all_gather(out_weight, "fsdp", axis=0, tiled=True),
    )
    (
        gain_full,
        in_full,
        conv_full,
        conv_shift,
        xproj_full,
        dt_full,
        dt_shift,
        alog_full,
        skip_full,
        out_full,
    ) = gathered
    gain_value = gain_full.astype(jnp.float32)
    conv_taps = conv_full.astype(jnp.float32)
    conv_offset = conv_shift.astype(jnp.float32)
    dt_offset = dt_shift.astype(jnp.float32)
    decay_rate = -jnp.exp(alog_full.astype(jnp.float32))
    skip_value = skip_full.astype(jnp.float32)
    inner_width = in_full.shape[1] // 2
    rank_width = dt_full.shape[0]
    state_width = decay_rate.shape[0]
    length = tokens.shape[0]
    tap_valid, keep_mask = cluster_masks(cluster_lengths)
    inputs_full = tokens.astype(jnp.float32)
    mean_square = jnp.mean(inputs_full * inputs_full, axis=-1, keepdims=True)
    inverse_rms = lax.rsqrt(mean_square + epsilon)
    unit_rows = inputs_full * inverse_rms
    normed_low = (unit_rows * gain_value).astype(jnp.bfloat16)
    mixed_in = matmul(normed_low, in_full)
    inner_in = mixed_in[:, :inner_width]
    gate_in = mixed_in[:, inner_width:]
    padded = jnp.pad(inner_in, ((KCONV - 1, 0), (0, 0)))
    conv_out = jnp.zeros_like(inner_in) + conv_offset
    for offset in range(KCONV):
        lag_now = KCONV - 1 - offset
        conv_out = (
            conv_out
            + conv_taps[offset]
            * padded[offset : offset + length]
            * tap_valid[:, lag_now : lag_now + 1]
        )
    conv_act = silu_of(conv_out)
    act_low = conv_act.astype(jnp.bfloat16)
    projected = matmul(act_low, xproj_full)
    dt_rounded = projected[:, :rank_width].astype(jnp.bfloat16)
    b_mat = projected[:, rank_width : rank_width + state_width]
    c_mat = projected[:, rank_width + state_width :]
    dt_pre = matmul(dt_rounded, dt_full) + dt_offset
    step_size = jax.nn.softplus(dt_pre)
    drive = step_size * conv_act
    blocked = (
        to_blocks(step_size),
        to_blocks(drive),
        to_blocks(b_mat),
        to_blocks(c_mat),
        to_blocks(keep_mask),
    )
    block_count = length // BLOCK
    zeros_state = jnp.zeros((block_count, state_width, inner_width), jnp.float32)

    def local_step(carried_in, inputs):
        carried, through = carried_in
        step_t, drive_t, b_t, c_t, keep_t = inputs
        factor = decay_factor(step_t, keep_t, decay_rate)
        carried = factor * carried + b_t[:, :, None] * drive_t[:, None, :]
        return ((carried, through * factor), None)

    (local_end, through), unused = lax.scan(
        local_step, (zeros_state, jnp.ones_like(zeros_state)), blocked
    )
    unused_total, reached = lax.associative_scan(chained, (through, local_end))
    starts = jnp.concatenate([zeros_state[:1], reached[:-1]], axis=0)

    def emit_only(carried, inputs):
        step_t, drive_t, b_t, c_t, keep_t = inputs
        factor = decay_factor(step_t, keep_t, decay_rate)
        updated = factor * carried + b_t[:, :, None] * drive_t[:, None, :]
        return (updated, jnp.sum(c_t[:, :, None] * updated, axis=1))

    def replay_step(carried, inputs):
        step_t, drive_t, b_t, c_t, keep_t = inputs
        factor = decay_factor(step_t, keep_t, decay_rate)
        return (factor * carried + b_t[:, :, None] * drive_t[:, None, :], carried)

    unused_last, scanned_blocks = lax.scan(emit_only, starts, blocked)
    scanned = from_blocks(scanned_blocks)
    with_skip = scanned + skip_value * conv_act
    gate_act = silu_of(gate_in)
    gated_low = (with_skip * gate_act).astype(jnp.bfloat16)
    result = inputs_full + matmul(gated_low, out_full)
    output = result.astype(jnp.bfloat16)
    out_grad = left_inner(gated_low, cotangent)
    gated_grad = right_inner(cotangent, out_full)
    skip_part = gated_grad * gate_act
    gate_grad = gated_grad * with_skip * silu_slope(gate_in)
    skip_grad = jnp.sum(skip_part * conv_act, axis=0)
    unused_end, prev_stack = lax.scan(replay_step, starts, blocked)
    dy_blocked = to_blocks(skip_part)
    act_blocked = to_blocks(conv_act)

    def adjoint_local(carried_in, inputs):
        step_t, drive_t, b_t, c_t, keep_t, dy_t = inputs
        factor = decay_factor(step_t, keep_t, decay_rate)
        adjoint = c_t[:, :, None] * dy_t[:, None, :] + carried_in
        return (factor * adjoint, None)

    local_out, unused = lax.scan(adjoint_local, zeros_state, blocked + (dy_blocked,), reverse=True)
    unused_total, back_reached = lax.associative_scan(
        chained, (jnp.flip(through, 0), jnp.flip(local_out, 0))
    )
    incoming = jnp.flip(jnp.concatenate([zeros_state[:1], back_reached[:-1]], axis=0), 0)

    def adjoint_step(carried_in, inputs):
        arriving, rate_grad = carried_in
        prev_t, step_t, drive_t, b_t, c_t, keep_t, dy_t, act_t = inputs
        factor = decay_factor(step_t, keep_t, decay_rate)
        adjoint = c_t[:, :, None] * dy_t[:, None, :] + arriving
        state_now = factor * prev_t + b_t[:, :, None] * drive_t[:, None, :]
        c_grad_t = jnp.sum(dy_t[:, None, :] * state_now, axis=2)
        decay_part = adjoint * prev_t * factor
        rate_grad = rate_grad + jnp.sum(decay_part * step_t[:, None, :], axis=0)
        input_part = jnp.sum(adjoint * b_t[:, :, None], axis=1)
        step_grad_t = jnp.sum(decay_part * decay_rate[None], axis=1) + input_part * act_t
        b_grad_t = jnp.sum(adjoint * drive_t[:, None, :], axis=2)
        act_grad_t = input_part * step_t
        return ((factor * adjoint, rate_grad), (step_grad_t, act_grad_t, b_grad_t, c_grad_t))

    rate_zero = jnp.zeros((state_width, inner_width), jnp.float32)
    (unused_first, rate_grad), (step_grad_b, act_scan_b, b_grad_b, c_grad_b) = lax.scan(
        adjoint_step,
        (incoming, rate_zero),
        (prev_stack,) + blocked + (dy_blocked, act_blocked),
        reverse=True,
    )
    a_log_grad = rate_grad * decay_rate
    step_grad = from_blocks(step_grad_b)
    act_scan = from_blocks(act_scan_b)
    b_grad = from_blocks(b_grad_b)
    c_grad = from_blocks(c_grad_b)
    pre_grad = step_grad * jax.nn.sigmoid(dt_pre)
    dt_bias_grad = jnp.sum(pre_grad, axis=0)
    pre_low = pre_grad.astype(jnp.bfloat16)
    dt_weight_grad = left_inner(dt_rounded, pre_low)
    rank_grad = right_inner(pre_low, dt_full)
    proj_grad = jnp.concatenate([rank_grad, b_grad, c_grad], axis=1).astype(jnp.bfloat16)
    xproj_grad = left_inner(act_low, proj_grad)
    act_grad = right_inner(proj_grad, xproj_full) + skip_part * skip_value + act_scan
    conv_grad = act_grad * silu_slope(conv_out)
    conv_bias_grad = jnp.sum(conv_grad, axis=0)
    inner_grad = jnp.zeros_like(inner_in)
    tap_grads = []
    for offset in range(KCONV):
        lag_now = KCONV - 1 - offset
        masked = conv_grad * tap_valid[:, lag_now : lag_now + 1]
        tap_grads.append(jnp.sum(masked * padded[offset : offset + length], axis=0))
        inner_grad = (
            inner_grad + conv_taps[offset] * jnp.pad(masked, ((0, lag_now), (0, 0)))[lag_now:]
        )
    conv_weight_grad = jnp.stack(tap_grads)
    mixed_grad = jnp.concatenate([inner_grad, gate_grad], axis=1).astype(jnp.bfloat16)
    in_grad = left_inner(normed_low, mixed_grad)
    normed_grad = right_inner(mixed_grad, in_full)
    gain_grad = jnp.sum(normed_grad * unit_rows, axis=0)
    scaled = normed_grad * gain_value
    input_grad = cotangent.astype(jnp.float32) + inverse_rms * (
        scaled - unit_rows * jnp.mean(scaled * unit_rows, axis=-1, keepdims=True)
    )
    shares = (
        lax.psum_scatter(
            gain_grad.astype(jnp.bfloat16), "fsdp", scatter_dimension=0, tiled=True
        ).astype(jnp.float32),
        lax.psum_scatter(
            in_grad.astype(jnp.bfloat16), "fsdp", scatter_dimension=0, tiled=True
        ).astype(jnp.float32),
        lax.psum_scatter(
            conv_weight_grad.astype(jnp.bfloat16), "fsdp", scatter_dimension=1, tiled=True
        ).astype(jnp.float32),
        lax.psum_scatter(
            conv_bias_grad.astype(jnp.bfloat16), "fsdp", scatter_dimension=0, tiled=True
        ).astype(jnp.float32),
        lax.psum_scatter(
            xproj_grad.astype(jnp.bfloat16), "fsdp", scatter_dimension=0, tiled=True
        ).astype(jnp.float32),
        lax.psum_scatter(
            dt_weight_grad.astype(jnp.bfloat16), "fsdp", scatter_dimension=1, tiled=True
        ).astype(jnp.float32),
        lax.psum_scatter(
            dt_bias_grad.astype(jnp.bfloat16), "fsdp", scatter_dimension=0, tiled=True
        ).astype(jnp.float32),
        lax.psum_scatter(
            a_log_grad.astype(jnp.bfloat16), "fsdp", scatter_dimension=1, tiled=True
        ).astype(jnp.float32),
        lax.psum_scatter(
            skip_grad.astype(jnp.bfloat16), "fsdp", scatter_dimension=0, tiled=True
        ).astype(jnp.float32),
        lax.psum_scatter(
            out_grad.astype(jnp.bfloat16), "fsdp", scatter_dimension=0, tiled=True
        ).astype(jnp.float32),
    )
    totals = lax.psum(
        (
            shares[0],
            shares[1],
            shares[2],
            shares[3],
            shares[4],
            shares[5],
            shares[6],
            shares[7],
            shares[8],
            shares[9],
        ),
        "dp",
    )
    return (
        output,
        input_grad,
        totals[0],
        totals[1],
        totals[2],
        totals[3],
        totals[4],
        totals[5],
        totals[6],
        totals[7],
        totals[8],
        totals[9],
    )


def solution(mesh):
    in_specs = (
        P(("dp", "fsdp"), None),
        P(("dp", "fsdp"), None),
        P("fsdp"),
        P("fsdp", None),
        P(None, "fsdp"),
        P("fsdp"),
        P("fsdp", None),
        P(None, "fsdp"),
        P("fsdp"),
        P(None, "fsdp"),
        P("fsdp"),
        P("fsdp", None),
        P(("dp", "fsdp"), None),
    )
    out_specs = (
        P(("dp", "fsdp"), None),
        P(("dp", "fsdp"), None),
        P("fsdp"),
        P("fsdp", None),
        P(None, "fsdp"),
        P("fsdp"),
        P("fsdp", None),
        P(None, "fsdp"),
        P("fsdp"),
        P(None, "fsdp"),
        P("fsdp"),
        P("fsdp", None),
    )
    return jax.shard_map(body, mesh=mesh, in_specs=in_specs, out_specs=out_specs, check_vma=False)
```

profile of v0, /device:TPU:0, one launch (start us, length us, event | category | flops | bytes accessed | tf_op | source)
XLA Modules:
  0.0 1596.7 jit_solution(5971714295107977627)
XLA Ops:
  9.4 6.0 all-gather.1
  41.6 5.8 all_gather.37
  47.5 7.9 all_gather.35
  55.4 9.3 all_gather.34
  65.2 9.4 all-gather.7.cloned.1.call-done
  74.6 7.1 fusion.51
  88.2 22.4 %all-gather.9.cloned.1.call-done = bf16[2048,1024]{1,0:T(8,128)(2,1)} async-done(((bf16[512,1024]{1,0:T(8,128)(2,1)}), bf16[2048,1024]{1,0:T(8,128)(2,1)}) %all-gather.9.cloned.1.call-update) | async-done | bytes 4194320 | tf_op jit(solution)/shard_map/all_gather | solution.py:97
  110.7 18.3 %multiply_reduce_fusion.5 = (bf16[2048]{0:T(1024)(128)(2,1)}, f32[512,2048]{1,0:T(8,128)}, f32[512,2048]{1,0:T(8,128)}, f32[512,2048]{1,0:T(8,128)}, f32[512,2048]{1,0:T(8,128)}) fusion(f32[512,4096]{1,0:T(8,128)} %copy-done.3, f32[512]{0:T(512)S(1)} %bitcast.230, f32[512,2048]{1,0:T(8,128)} %slice.410, f32[2048]{0:T(1024)S(1)} %bitcast.224, ...), kind=kOutput, calls=%fused_computation.81 | convolution fusion | flops 2171598848 | bytes 30461952 | tf_op jit(solution)/shard_map/dot_general | solution.py:25
  133.1 6.8 fusion.71
  139.9 8.1 copy_bitcast_fusion.2
  148.0 120.3 %while.79 = (s32[]{:T(128)}, f32[32,16,2048]{2,1,0:T(8,128)}, f32[32,16,2048]{2,1,0:T(8,128)}, f32[16,32]{1,0:T(8,128)S(1)}, f32[16,32,2048]{2,1,0:T(8,128)}, /*...) while((s32[]{:T(128)}, f32[32,16,2048]{2,1,0:T(8,128)}, ...), condition=%wide.region_4.5_spmd.clone, body=%wide.region_3.4_spmd.clone.sunk | while | flops 8388611 | bytes 18487800 | solution.py:166
  154.6 6.5 select_multiply_fusion.3
  162.2 6.5 select_multiply_fusion.3
  169.9 6.5 select_multiply_fusion.3
  177.5 6.5 select_multiply_fusion.3
  185.2 6.5 select_multiply_fusion.3
  192.8 6.5 select_multiply_fusion.3
  200.5 6.5 select_multiply_fusion.3
  208.1 6.5 select_multiply_fusion.3
  215.8 6.5 select_multiply_fusion.3
  223.4 6.5 select_multiply_fusion.3
  231.1 6.5 select_multiply_fusion.3
  238.7 6.5 select_multiply_fusion.3
  246.4 6.5 select_multiply_fusion.3
  254.1 6.5 select_multiply_fusion.3
  261.7 6.5 select_multiply_fusion.3
  268.2 6.7 fusion.73
  319.3 11.6 copy_bitcast_fusion
  330.9 101.7 %while.80 = (s32[]{:T(128)}, f32[32,16,2048]{2,1,0:T(8,128)}, f32[16,32]{1,0:T(8,128)S(1)}, f32[16,32,2048]{2,1,0:T(8,128)}, f32[16,2048]{1,0:T(8,128)S(1)}, /*i...) while((s32[]{:T(128)}, f32[32,16,2048]{2,1,0:T(8,128)}, ...), condition=%wide.region_9.10_spmd.clone, body=%wide.region_8.9_spmd.clone.sunk | while | flops 6291460 | bytes 10099207 | solution.py:205
  465.9 7.4 pad.227
  475.0 7.7 pad.131
  493.8 177.9 %while.78 = (s32[]{:T(128)}, f32[32,16,2048]{2,1,0:T(8,128)}, f32[16,32,16,2048]{3,2,1,0:T(8,128)}, f32[16,32]{1,0:T(8,128)S(1)}, f32[16,32,2048]{2,1,0:T(8,128)...) while((s32[]{:T(128)}, f32[32,16,2048]{2,1,0:T(8,128)}, ...), condition=%wide.region_11.12_spmd, body=%wide.region_10.11_spmd.sunk | while | flops 5242882 | bytes 18488296 | solution.py:195
  683.8 11.4 pad.228
  699.0 7.3 pad.133
  722.5 218.8 %while.81 = (s32[]{:T(128)}, f32[32,16,2048]{2,1,0:T(8,128)}, f32[16,2048]{1,0:T(8,128)S(1)}, f32[16,32,2048]{2,1,0:T(8,128)}, f32[16,32,2048]{2,1,0:T(8,128)}, ...) while((s32[]{:T(128)}, f32[32,16,2048]{2,1,0:T(8,128)}, ...), condition=%wide.region_18.19_spmd.clone, body=%wide.region_12.18_spmd.clone.sunk | while | flops 21068804 | bytes 17742436 | solution.py:227
  725.3 8.9 multiply_reduce_fusion.13
  739.0 8.9 multiply_reduce_fusion.13
  752.7 8.9 multiply_reduce_fusion.13
  766.4 8.9 multiply_reduce_fusion.13
  780.1 8.9 multiply_reduce_fusion.13
  793.8 8.9 multiply_reduce_fusion.13
  807.4 8.9 multiply_reduce_fusion.13
  821.0 8.9 multiply_reduce_fusion.13
  834.7 8.9 multiply_reduce_fusion.13
  848.4 8.9 multiply_reduce_fusion.13
  862.0 8.9 multiply_reduce_fusion.13
  875.7 8.9 multiply_reduce_fusion.13
  889.4 8.9 multiply_reduce_fusion.13
  903.0 8.9 multiply_reduce_fusion.13
  916.7 8.9 multiply_reduce_fusion.13
  930.3 8.9 multiply_reduce_fusion.13
  951.6 119.0 %while.77 = (s32[]{:T(128)}, f32[32,16,2048]{2,1,0:T(8,128)}, f32[16,32,2048]{2,1,0:T(8,128)}, f32[16,32]{1,0:T(8,128)S(1)}, f32[16,32,2048]{2,1,0:T(8,128)}, /*...) while((s32[]{:T(128)}, f32[32,16,2048]{2,1,0:T(8,128)}, ...), condition=%wide.region_7.8_spmd, body=%wide.region_5.7_spmd.sunk | while | flops 7274498 | bytes 10892273 | solution.py:183
  1070.6 6.7 copy.85
  1081.9 16.7 %multiply_reduce_fusion.9 = (bf16[2048]{0:T(1024)(128)(2,1)S(1)}, bf16[2048]{0:T(1024)(128)(2,1)S(1)}, bf16[2048]{0:T(1024)(128)(2,1)S(1)}, f32[512,2048]{1,0:T(...) fusion(f32[512,2048]{1,0:T(8,128)} %slice.410, f32[512]{0:T(512)S(1)} %bitcast.236, ...), kind=kOutput, calls=%fused_computation.85 | convolution fusion | flops 222586880 | bytes 34072576 | tf_op jit(solution)/shard_map/dot_general | solution.py:25
  1098.8 16.3 %fusion.67 = (bf16[2048]{0:T(1024)(128)(2,1)S(1)}, bf16[2048]{0:T(1024)(128)(2,1)S(1)}, bf16[512,2048]{1,0:T(8,128)(2,1)}, bf16[512,2048]{1,0:T(8,128)(2,1)}, bf16[512,2048]{1,0:T(8,128)(2,1)}) fusion(f32[512,2048]{1,0:T(8,128)} %get-tuple-element.1060, f32[512,4096]{1,0:T(8,128)} %copy-done.3, f32[512]{0:T(512)S(1)} %bitcast.231, ...), kind=kLoop, calls=%fused_computation.202 | loop fusion | flops 28307456 | bytes 44091392 | tf_op jit(solution)/shard_map/reduce_sum | solution.py:247
  1122.0 5.6 convolution_convert_fusion.1
  1128.9 9.5 convolution_convert_fusion
  1140.9 10.7 fusion.35
  1151.6 10.2 all-reduce.31
  1170.4 12.6 reduce-scatter.13.cloned.1.call-done
  1183.0 23.2 %reduce-scatter.11.cloned.1.call-done = bf16[512,96]{0,1:T(8,128)(2,1)} async-done(((bf16[2048,96]{0,1:T(8,128)(2,1)}), bf16[512,96]{0,1:T(8,128)(2,1)}) %reduce-scatter.11.cloned.1.call-update) | async-done | bytes 98320 | tf_op jit(solution)/shard_map/reduce_scatter | solution.py:279
  1206.2 47.7 %reduce-scatter.17.cloned.1.call-done = bf16[512,1024]{1,0:T(8,128)(2,1)} async-done(((bf16[2048,1024]{1,0:T(8,128)(2,1)}), bf16[512,1024]{1,0:T(8,128)(2,1)}) %reduce-scatter.17.cloned.1.call-update) | async-done | bytes 1048592 | tf_op jit(solution)/shard_map/reduce_scatter | solution.py:294
  1253.9 74.0 %reduce-scatter.9.cloned.1.call-done = bf16[256,4096]{1,0:T(8,128)(2,1)} async-done(((bf16[1024,4096]{1,0:T(8,128)(2,1)}), bf16[256,4096]{1,0:T(8,128)(2,1)}) %reduce-scatter.9.cloned.1.call-update) | async-done | bytes 2097168 | tf_op jit(solution)/shard_map/reduce_scatter | solution.py:270
  1327.9 261.5 %all-reduce.33 = (f32[256]{0:T(256)}, f32[256,4096]{1,0:T(8,128)}, f32[4,512]{1,0:T(4,128)}, f32[512]{0:T(512)}, f32[512,96]{0,1:T(8,128)}, /*index=5*/f32[64,51...) all-reduce(f32[256]{0:T(256)S(1)} %dynamic-slice_convert_fusion.3, ...), channel_id=1, replica_groups=mesh['dp'=8,'fsdp'=4] {'dp'}, use_global_device_ids=true, to_apply=%region_22.23 | all-reduce | flops 1666816 | bytes 10004480 | tf_op jit(solution)/shard_map/psum | solution.py:298
  (671 shorter events, 689.6 us)
Async XLA Ops:
  7.2 57.6 %copy-start.18 = (bf16[512,1024]{1,0:T(8,128)(2,1)S(1)}, bf16[512,1024]{1,0:T(8,128)(2,1)}, u32[]{:S(2)}) copy-start(bf16[512,1024]{1,0:T(8,128)(2,1)} %param.23) | copy-start | bytes 3145732
  7.2 67.4 %all-gather.7.cloned.1.call-start = ((), (), s32[]{:S(2)}) async-start(), calls=%async_computation.6 | async-start | bytes 10485760 | tf_op jit(solution)/shard_map/all_gather | solution.py:89
  7.9 102.7 %all-gather.9.cloned.1.call-start = ((), (), s32[]{:S(2)}) async-start(), calls=%async_computation.7 | async-start | bytes 5242880 | tf_op jit(solution)/shard_map/all_gather | solution.py:97
  8.7 1160.8 %reduce-scatter.19.cloned.1.call-start = ((), (), s32[]{:S(2)}) async-start(), calls=%async_computation.13 | async-start | bytes 655360
  15.5 66.2 %copy-start.48 = (f32[4,1,256]{2,1,0:T(1,128)}, f32[4,1,256]{2,1,0:T(1,128)S(1)}, u32[]{:S(2)}) copy-start(f32[4,1,256]{2,1,0:T(1,128)S(1)} %convert_element_type.152) | copy-start | bytes 12292
  28.5 104.5 %copy-start.37 = (f32[4,1,512]{2,1,0:T(1,128)}, f32[4,1,512]{2,1,0:T(1,128)S(1)}, u32[]{:S(2)}) copy-start(f32[4,1,512]{2,1,0:T(1,128)S(1)} %convert_element_type.153) | copy-start | bytes 24580
  47.5 17.7 %copy-start.30 = (bf16[16,2048]{1,0:T(8,128)(2,1)}, bf16[16,2048]{1,0:T(8,128)(2,1)S(1)}, u32[]{:S(2)}) copy-start(bf16[16,2048]{1,0:T(8,128)(2,1)S(1)} %all_gather.37) | copy-start | bytes 196612
  55.4 77.7 %copy-start.21 = (bf16[64,2048]{1,0:T(8,128)(2,1)}, bf16[64,2048]{1,0:T(8,128)(2,1)S(1)}, u32[]{:S(2)}) copy-start(bf16[64,2048]{1,0:T(8,128)(2,1)S(1)} %all_gather.35) | copy-start | bytes 786436
  64.7 64.3 %copy-start.24 = (bf16[2048,96]{0,1:T(8,128)(2,1)}, bf16[2048,96]{0,1:T(8,128)(2,1)S(1)}, u32[]{:S(2)}) copy-start(bf16[2048,96]{0,1:T(8,128)(2,1)S(1)} %all_gather.34) | copy-start | bytes 1179652
  65.0 16.7 %copy-start.50 = (f32[512]{0:T(512)}, f32[512]{0:T(512)S(1)}, u32[]{:S(2)}) copy-start(f32[512]{0:T(512)S(1)} %add_rsqrt_fusion) | copy-start | bytes 6148
  65.1 45.6 %copy-start.52 = (f32[512,1]{0,1:T(1,128)}, f32[512,1]{0,1:T(1,128)S(1)}, u32[]{:S(2)}) copy-start(f32[512,1]{0,1:T(1,128)S(1)} %get-tuple-element.1055) | copy-start | bytes 6148
  65.1 45.6 %copy-start.55 = (f32[512,1]{0,1:T(1,128)}, f32[512,1]{0,1:T(1,128)S(1)}, u32[]{:S(2)}) copy-start(f32[512,1]{0,1:T(1,128)S(1)} %get-tuple-element.1054) | copy-start | bytes 6148
  65.1 45.6 %copy-start.57 = (f32[512,1]{0,1:T(1,128)}, f32[512,1]{0,1:T(1,128)S(1)}, u32[]{:S(2)}) copy-start(f32[512,1]{0,1:T(1,128)S(1)} %get-tuple-element.1056) | copy-start | bytes 6148
  65.1 45.6 %copy-start.59 = (f32[512,1]{0,1:T(1,128)}, f32[512,1]{0,1:T(1,128)S(1)}, u32[]{:S(2)}) copy-start(f32[512,1]{0,1:T(1,128)S(1)} %get-tuple-element.1057) | copy-start | bytes 6148
  65.2 45.5 %copy-start.40 = (f32[1,2048]{1,0:T(1,128)}, f32[1,2048]{1,0:T(1,128)S(1)}, u32[]{:S(2)}) copy-start(f32[1,2048]{1,0:T(1,128)S(1)} %get-tuple-element.1050) | copy-start | bytes 24580
  65.2 45.5 %copy-start.42 = (f32[1,2048]{1,0:T(1,128)}, f32[1,2048]{1,0:T(1,128)S(1)}, u32[]{:S(2)}) copy-start(f32[1,2048]{1,0:T(1,128)S(1)} %get-tuple-element.1051) | copy-start | bytes 24580
  65.2 45.5 %copy-start.44 = (f32[1,2048]{1,0:T(1,128)}, f32[1,2048]{1,0:T(1,128)S(1)}, u32[]{:S(2)}) copy-start(f32[1,2048]{1,0:T(1,128)S(1)} %get-tuple-element.1052) | copy-start | bytes 24580
  65.2 45.5 %copy-start.46 = (f32[1,2048]{1,0:T(1,128)}, f32[1,2048]{1,0:T(1,128)S(1)}, u32[]{:S(2)}) copy-start(f32[1,2048]{1,0:T(1,128)S(1)} %get-tuple-element.1053) | copy-start | bytes 24580
  81.7 4.0 copy-start.3
  85.7 25.0 %copy-start.28 = (bf16[512,1024]{1,0:T(8,128)(2,1)S(1)}, bf16[512,1024]{1,0:T(8,128)(2,1)}, u32[]{:S(2)}) copy-start(bf16[512,1024]{1,0:T(8,128)(2,1)} %param.35) | copy-start | bytes 3145732
  132.0 7.9 copy-start.26
  274.9 1.3 copy-start.8
  296.6 1.8 copy-start.9
  296.6 2.9 copy-start.35
  299.5 5.0 copy-start.17
  308.6 3.3 copy-start
  308.6 4.3 copy-start.4
  312.8 6.1 copy-start.36
  432.6 2.7 copy-start.29
  432.6 2.9 copy-start.11
  432.6 3.6 copy-start.12
  437.4 1.4 copy-start.14
  458.6 5.2 copy-start.1
  461.4 4.6 copy-start.10
  465.3 8.0 copy-start.32
  493.8 177.9 %copy-start.20 = (f32[7,16,2048]{2,1,0:T(8,128)S(1)}, f32[7,16,2048]{2,1,0:T(8,128)}, u32[]{:S(2)}) copy-start(f32[7,16,2048]{2,1,0:T(8,128)} %fusion.45) | copy-start | bytes 2752516
  493.8 177.9 %copy-start.34 = (f32[1,16,2048]{2,1,0:T(8,128)S(1)}, f32[1,16,2048]{2,1,0:T(8,128)}, u32[]{:S(2)}) copy-start(f32[1,16,2048]{2,1,0:T(8,128)} %slice.439) | copy-start | bytes 393220
  671.7 4.9 copy-start.16
  695.3 3.5 copy-start.33
  717.5 5.1 copy-start.15
  941.3 4.8 copy-start.6
  941.3 4.8 copy-start.38
  1070.6 6.7 copy-start.5
  1077.4 4.5 copy-start.25
  1077.4 4.5 copy-start.39
  1077.4 4.5 copy-start.56
  1077.4 4.5 copy-start.58
  1077.4 4.5 copy-start.60
  1081.9 16.8 %copy-start.2 = (f32[512,2048]{1,0:T(8,128)S(1)}, f32[512,2048]{1,0:T(8,128)}, u32[]{:S(2)}) copy-start(f32[512,2048]{1,0:T(8,128)} %get-tuple-element.986) | copy-start | bytes 12582916
  1081.9 16.8 %copy-start.41 = (f32[1,2048]{1,0:T(1,128)S(1)}, f32[1,2048]{1,0:T(1,128)}, u32[]{:S(2)}) copy-start(f32[1,2048]{1,0:T(1,128)} %copy-done.40) | copy-start | bytes 24580
  1081.9 16.8 %copy-start.43 = (f32[1,2048]{1,0:T(1,128)S(1)}, f32[1,2048]{1,0:T(1,128)}, u32[]{:S(2)}) copy-start(f32[1,2048]{1,0:T(1,128)} %copy-done.42) | copy-start | bytes 24580
  1081.9 16.8 %copy-start.45 = (f32[1,2048]{1,0:T(1,128)S(1)}, f32[1,2048]{1,0:T(1,128)}, u32[]{:S(2)}) copy-start(f32[1,2048]{1,0:T(1,128)} %copy-done.44) | copy-start | bytes 24580
  1081.9 16.8 %copy-start.47 = (f32[1,2048]{1,0:T(1,128)S(1)}, f32[1,2048]{1,0:T(1,128)}, u32[]{:S(2)}) copy-start(f32[1,2048]{1,0:T(1,128)} %copy-done.46) | copy-start | bytes 24580
  1081.9 16.8 %copy-start.53 = (f32[512,1]{0,1:T(1,128)S(1)}, f32[512,1]{0,1:T(1,128)}, u32[]{:S(2)}) copy-start(f32[512,1]{0,1:T(1,128)} %copy-done.52) | copy-start | bytes 6148
  1098.7 17.6 %copy-start.31 = (bf16[16,2048]{1,0:T(8,128)(2,1)S(1)}, bf16[16,2048]{1,0:T(8,128)(2,1)}, u32[]{:S(2)}) copy-start(bf16[16,2048]{1,0:T(8,128)(2,1)} %copy-done.30) | copy-start | bytes 196612
  1098.8 18.3 %copy-start.27 = (f32[512,96]{0,1:T(8,128)S(1)}, f32[512,96]{0,1:T(8,128)}, u32[]{:S(2)}) copy-start(f32[512,96]{0,1:T(8,128)} %copy-done.26) | copy-start | bytes 589828
  1116.3 54.1 %reduce-scatter.15.cloned.1.call-start = ((), (), s32[]{:S(2)}) async-start(), calls=%async_computation.11 | async-start | bytes 81920 | tf_op jit(solution)/shard_map/reduce_scatter | solution.py:288
  1117.0 66.0 %reduce-scatter.13.cloned.1.call-start = ((), (), s32[]{:S(2)}) async-start(), calls=%async_computation.10 | async-start | bytes 327680 | tf_op jit(solution)/shard_map/reduce_scatter | solution.py:282
  1118.3 3.7 copy-start.23
  1118.3 87.9 %reduce-scatter.11.cloned.1.call-start = ((), (), s32[]{:S(2)}) async-start(), calls=%async_computation.9 | async-start | bytes 491520 | tf_op jit(solution)/shard_map/reduce_scatter | solution.py:279
  1122.0 131.9 %reduce-scatter.17.cloned.1.call-start = ((), (), s32[]{:S(2)}) async-start(), calls=%async_computation.12 | async-start | bytes 5242880 | tf_op jit(solution)/shard_map/reduce_scatter | solution.py:294
  1127.7 200.2 %reduce-scatter.9.cloned.1.call-start = ((), (), s32[]{:S(2)}) async-start(), calls=%async_computation.8 | async-start | bytes 10485760 | tf_op jit(solution)/shard_map/reduce_scatter | solution.py:270
  1140.9 10.7 copy-start.54
  1161.8 4.3 copy-start.61
  (7 other events, 8.2 us)
Sparse Core Ops, SparseCore 0:
  9.6 65.0 all-gather.6
  76.2 34.4 all-gather.8
  1116.4 21.6 reduce-scatter.18
  1140.9 19.5 reduce-scatter.14
  1162.9 20.0 reduce-scatter.12
  1185.4 20.7 reduce-scatter.10
  1209.3 44.5 reduce-scatter.16
  1256.5 71.3 reduce-scatter.8
where the time goes:
time: 1610 us; the launch traced here: 1600 us
  other arithmetic  607 us (38%)
  local copies, waits for them, and re-layouts  371 us (23%)
  blocking collectives  323 us (20%)
  waiting for transfers between devices  191 us (12%)
  matrix products  86.5 us (5%)
  between operations  16.8 us (1%)
    psum x1, blocking collectives, body(): lax.psum((shares[0], shares[1], shares[2], shares[3], shares[4], shares[5...  262 us
    reduce_sum x16, other arithmetic, adjoint_step(): jnp.sum(decay_part * decay_rate[None], axis=1) + input_part * act_t  142 us
    mul x16, other arithmetic, local_step(): return ((carried, through * factor), None)  102 us
    add x16, other arithmetic, replay_step(): return (factor * carried + b_t[:, :, None] * drive_t[:, None, :], carried)  85.4 us
    mul x16, other arithmetic, adjoint_local(): return (factor * adjoint, None)  83.9 us
    reduce_sum x16, other arithmetic, emit_only(): return (updated, jnp.sum(c_t[:, :, None] * updated, axis=1))  78.6 us
    dynamic_update_slice x16, local copies, waits for them, and re-layouts, body(): unused_end, prev_stack = lax.scan(replay_step, starts, blocked)  75.1 us
    reduce_scatter x1, waiting for transfers between devices, body(): lax.psum_scatter(in_grad.astype(jnp.bfloat16), 'fsdp', scatter_dimension=...  74 us
  transfers between devices with their start and end apart: 8, of which 6 were waited for; matrix products, arithmetic and copies ran while one was open for 3% of the time, Pallas kernels for 0%

commit v1 on v0

v1 whole, which is shorter than its diff:
```python
import jax
import jax.numpy as jnp
import numpy as np
from jax import lax
from jax.experimental import pallas as pl
from jax.experimental.pallas import tpu as pltpu
from jax.sharding import PartitionSpec as P

KCONV = 4
LENGTH = 512
LOG2E = float(np.log2(np.e))
LN2 = float(np.log(2.0))
FAR = 1e30


epsilon = 1e-05


def matmul(former, latter):
    return jnp.dot(former, latter, preferred_element_type=jnp.float32)


def left_inner(former, latter):
    return lax.dot_general(
        former, latter, (((0,), (0,)), ((), ())), preferred_element_type=jnp.float32
    )


def right_inner(former, latter):
    return lax.dot_general(
        former, latter, (((1,), (1,)), ((), ())), preferred_element_type=jnp.float32
    )


def silu_of(values):
    return values * jax.nn.sigmoid(values)


def silu_slope(values):
    logistic = jax.nn.sigmoid(values)
    return logistic * (1.0 + values * (1.0 - logistic))


def cluster_masks(lengths):
    cluster_ends = jnp.cumsum(lengths, axis=-1)
    starts = cluster_ends - lengths
    positions = jnp.arange(LENGTH, dtype=jnp.int32)
    before = starts[:, None, :] <= positions[None, :, None]
    segment_start = jnp.max(jnp.where(before, starts[:, None, :], 0), axis=-1)
    keep_mask = (positions[None, :] > segment_start).astype(jnp.float32)
    lag_index = jnp.arange(KCONV, dtype=jnp.int32)
    tap_valid = (
        positions[None, :, None] - lag_index[None, None, :] >= segment_start[:, :, None]
    ).astype(jnp.float32)
    return (tap_valid[0], keep_mask[0])

LANE = 128
NS = 16
TC = 32
CGF = 1024
CGB = 512


def bcast(ref, i, row):
    v = ref[i, pl.ds(row, 8, stride=0), :]
    return jnp.concatenate([v, v], axis=0)


def stage(src, dst):
    for i in range(dst.shape[0]):
        dst[i] = src[:, i * LANE:(i + 1) * LANE]


def fold(src, i):
    s = [src[i, pl.ds(q, 8, stride=8), :] for q in range(8)]
    return ((s[0] + s[1]) + (s[2] + s[3])) + ((s[4] + s[5]) + (s[6] + s[7]))


def fwd_kernel(dt_ref, dr_ref, b_ref, c_ref, a_ref, y_ref, hs_ref, part, dts, drs, hst):
    cg = dt_ref.shape[1]
    tiles = cg // LANE
    tc = dt_ref.shape[0]

    @pl.when(pl.program_id(1) == 0)
    def _():
        hst[...] = jnp.zeros_like(hst)

    hs_ref[0] = hst[...]
    stage(dt_ref, dts)
    stage(dr_ref, drs)

    def group(g, carry):
        t0 = pl.multiple_of(g * 8, 8)
        hs = list(carry)
        for k in range(8):
            bt = b_ref[t0 + k]
            ct = c_ref[t0 + k]
            for i in range(tiles):
                ln = slice(i * LANE, (i + 1) * LANE)
                d = bcast(dts, i, t0 + k)
                u = bcast(drs, i, t0 + k)
                a = jnp.exp2(d * a_ref[:, ln])
                h = a * hs[i] + bt * u
                hs[i] = h
                p = ct * h
                part[i, k * 8:(k + 1) * 8, :] = p[:8] + p[8:]
        for i in range(tiles):
            ln = slice(i * LANE, (i + 1) * LANE)
            y_ref[pl.ds(t0, 8), ln] = fold(part, i)
        return tuple(hs)

    init = tuple(hst[:, i * LANE:(i + 1) * LANE] for i in range(tiles))
    out = lax.fori_loop(0, tc // 8, group, init)
    for i in range(tiles):
        hst[:, i * LANE:(i + 1) * LANE] = out[i]


def scan_forward(dt, dr, bx, cx, a2, tc=TC, cg=CGF):
    t, c = dt.shape
    nt, nc = t // tc, c // cg
    return pl.pallas_call(
        fwd_kernel,
        grid=(nc, nt),
        in_specs=[
            pl.BlockSpec((tc, cg), lambda j, i: (i, j)),
            pl.BlockSpec((tc, cg), lambda j, i: (i, j)),
            pl.BlockSpec((tc, NS, LANE), lambda j, i: (i, 0, 0)),
            pl.BlockSpec((tc, NS, LANE), lambda j, i: (i, 0, 0)),
            pl.BlockSpec((NS, cg), lambda j, i: (0, j)),
        ],
        out_specs=[
            pl.BlockSpec((tc, cg), lambda j, i: (i, j)),
            pl.BlockSpec((1, NS, cg), lambda j, i: (i, 0, j)),
        ],
        out_shape=[
            jax.ShapeDtypeStruct((t, c), jnp.float32),
            jax.ShapeDtypeStruct((nt, NS, c), jnp.float32),
        ],
        scratch_shapes=[pltpu.VMEM((cg // LANE, 64, LANE), jnp.float32)] + [pltpu.VMEM((cg // LANE, tc, LANE), jnp.float32)] * 2 + [pltpu.VMEM((NS, cg), jnp.float32)],
        name="scan_forward",
    )(dt, dr, bx, cx, a2)


def bwd_kernel(dt_ref, dr_ref, dy_ref, b_ref, c_ref, a_ref, hs_ref,
               za_ref, gb_ref, db_ref, dc_ref, rate_ref, asc, hsc, pz, pg, dts, drs, dys, gst, rst):
    cg = dt_ref.shape[1]
    tiles = cg // LANE
    tc = dt_ref.shape[0]
    j = pl.program_id(0)
    i_t = pl.program_id(1)
    nt = pl.num_programs(1)

    @pl.when(i_t == 0)
    def _():
        gst[...] = jnp.zeros_like(gst)
        rst[...] = jnp.zeros_like(rst)

    stage(dt_ref, dts)
    stage(dr_ref, drs)
    stage(dy_ref, dys)
    lanes = [slice(i * LANE, (i + 1) * LANE) for i in range(tiles)]

    def fgroup(g, carry):
        t0 = pl.multiple_of(g * 8, 8)
        hs = list(carry)
        for k in range(8):
            bt = b_ref[t0 + k]
            for i in range(tiles):
                ln = lanes[i]
                d = bcast(dts, i, t0 + k)
                u = bcast(drs, i, t0 + k)
                a = jnp.exp2(d * a_ref[:, ln])
                asc[t0 + k, :, ln] = a
                hsc[t0 + k, :, ln] = hs[i]
                hs[i] = a * hs[i] + bt * u
        return tuple(hs)

    out = lax.fori_loop(0, tc // 8, fgroup, tuple(hs_ref[0, :, ln] for ln in lanes))
    for i in range(tiles):
        hsc[tc, :, lanes[i]] = out[i]

    base = pl.multiple_of((nt - 1 - i_t) * tc, tc)
    first = j == 0

    def bgroup(gi, carry):
        g = tc // 8 - 1 - gi
        t0 = pl.multiple_of(g * 8, 8)
        gs = list(carry[0])
        rs = list(carry[1])
        for k in range(7, -1, -1):
            bt = b_ref[t0 + k]
            ct = c_ref[t0 + k]
            accb = None
            for i in range(tiles):
                ln = lanes[i]
                d = bcast(dts, i, t0 + k)
                u = bcast(drs, i, t0 + k)
                w = bcast(dys, i, t0 + k)
                hnow = hsc[t0 + k + 1, :, ln]
                hprev = hsc[t0 + k, :, ln]
                a = asc[t0 + k, :, ln]
                gg = ct * w + gs[i]
                ga = gg * a
                z = ga * hprev
                rs[i] = rs[i] + z * d
                gs[i] = ga
                pa = z * a_ref[:, ln]
                pz[i, k * 8:(k + 1) * 8, :] = pa[:8] + pa[8:]
                pb = gg * bt
                pg[i, k * 8:(k + 1) * 8, :] = pb[:8] + pb[8:]
                vb = gg * u
                vc = w * hnow
                accb = vb if accb is None else accb + vb
                accc = vc if i == 0 else accc + vc
            row = base + t0 + k

            @pl.when(first)
            def _():
                db_ref[row] = accb
                dc_ref[row] = accc

            @pl.when(jnp.logical_not(first))
            def _():
                db_ref[row] = db_ref[row] + accb
                dc_ref[row] = dc_ref[row] + accc
        for i in range(tiles):
            ln = lanes[i]
            za_ref[pl.ds(t0, 8), ln] = fold(pz, i)
            gb_ref[pl.ds(t0, 8), ln] = fold(pg, i)
        return tuple(gs), tuple(rs)

    gs, rs = lax.fori_loop(0, tc // 8, bgroup, (tuple(gst[:, ln] for ln in lanes), tuple(rst[:, ln] for ln in lanes)))
    for i in range(tiles):
        gst[:, lanes[i]] = gs[i]
        rst[:, lanes[i]] = rs[i]

    @pl.when(i_t == nt - 1)
    def _():
        rate_ref[...] = rst[...]


def scan_backward(dt, dr, dy, bx, cx, a2, hs, tc=TC, cg=CGB):
    t, c = dt.shape
    nt, nc = t // tc, c // cg
    row = pl.BlockSpec((tc, cg), lambda j, i: (nt - 1 - i, j))
    bc = pl.BlockSpec((tc, NS, LANE), lambda j, i: (nt - 1 - i, 0, 0))
    full = pl.BlockSpec((t, NS, LANE), lambda j, i: (0, 0, 0))
    return pl.pallas_call(
        bwd_kernel,
        grid=(nc, nt),
        in_specs=[row, row, row, bc, bc, pl.BlockSpec((NS, cg), lambda j, i: (0, j)),
                  pl.BlockSpec((1, NS, cg), lambda j, i: (nt - 1 - i, 0, j))],
        out_specs=[row, row, full, full, pl.BlockSpec((NS, cg), lambda j, i: (0, j))],
        out_shape=[
            jax.ShapeDtypeStruct((t, c), jnp.float32),
            jax.ShapeDtypeStruct((t, c), jnp.float32),
            jax.ShapeDtypeStruct((t, NS, LANE), jnp.float32),
            jax.ShapeDtypeStruct((t, NS, LANE), jnp.float32),
            jax.ShapeDtypeStruct((NS, c), jnp.float32),
        ],
        scratch_shapes=[
            pltpu.VMEM((tc, NS, cg), jnp.float32), pltpu.VMEM((tc + 1, NS, cg), jnp.float32),
            pltpu.VMEM((cg // LANE, 64, LANE), jnp.float32), pltpu.VMEM((cg // LANE, 64, LANE), jnp.float32),
            pltpu.VMEM((cg // LANE, tc, LANE), jnp.float32), pltpu.VMEM((cg // LANE, tc, LANE), jnp.float32), pltpu.VMEM((cg // LANE, tc, LANE), jnp.float32),
            pltpu.VMEM((NS, cg), jnp.float32), pltpu.VMEM((NS, cg), jnp.float32),
        ],
        compiler_params=pltpu.CompilerParams(vmem_limit_bytes=56 << 20),
        name="scan_backward",
    )(dt, dr, dy, bx, cx, a2, hs)


def pack_small(gain, conv_w, conv_b, xproj, dt_w, dt_b, alog, skip):
    width = conv_b.shape[-1]
    gain_row = jnp.pad(gain[None], ((0, 0), (0, width - gain.shape[0])))
    return jnp.concatenate(
        [xproj.T, dt_w, alog, conv_w, conv_b[None], dt_b[None], skip[None], gain_row], axis=0
    )


def body(
    tokens,
    cluster_lengths,
    norm_gain,
    in_weight,
    conv_weight,
    conv_bias,
    xproj_weight,
    dt_weight,
    dt_bias,
    a_log,
    skip_gain,
    out_weight,
    cotangent,
):
    low = jnp.bfloat16
    gain_shard = norm_gain.shape[0]
    width = conv_bias.shape[0]
    packed = pack_small(norm_gain, conv_weight, conv_bias, xproj_weight, dt_weight, dt_bias, a_log, skip_gain)
    in_full = lax.all_gather(in_weight, "fsdp", axis=0, tiled=True)
    small = lax.all_gather(packed, "fsdp", axis=0)
    out_full = lax.all_gather(out_weight, "fsdp", axis=0, tiled=True)
    shards = small.shape[0]
    xw, rank, state = xproj_weight.shape[1], dt_weight.shape[0], a_log.shape[0]
    rows = jnp.moveaxis(small, 0, 1).reshape(small.shape[1], shards * width)
    xproj_t = rows[:xw]
    dt_full = rows[xw : xw + rank]
    at = xw + rank
    alog_full = rows[at : at + state]
    at += state
    conv_taps = rows[at : at + KCONV].astype(jnp.float32)
    at += KCONV
    conv_offset = rows[at].astype(jnp.float32)
    dt_offset = rows[at + 1].astype(jnp.float32)
    skip_value = rows[at + 2].astype(jnp.float32)
    gain_value = small[:, at + 3, :gain_shard].reshape(-1).astype(jnp.float32)
    decay_rate = -jnp.exp(alog_full.astype(jnp.float32))
    inner_width = shards * width
    length = tokens.shape[0]
    tap_valid, keep_mask = cluster_masks(cluster_lengths)
    inputs_full = tokens.astype(jnp.float32)
    mean_square = jnp.mean(inputs_full * inputs_full, axis=-1, keepdims=True)
    inverse_rms = lax.rsqrt(mean_square + epsilon)
    unit_rows = inputs_full * inverse_rms
    normed_low = (unit_rows * gain_value).astype(low)
    mixed_in = matmul(normed_low, in_full)
    inner_in = mixed_in[:, :inner_width]
    gate_in = mixed_in[:, inner_width:]
    padded = jnp.pad(inner_in, ((KCONV - 1, 0), (0, 0)))
    conv_out = jnp.zeros_like(inner_in) + conv_offset
    for offset in range(KCONV):
        lag_now = KCONV - 1 - offset
        conv_out = (
            conv_out
            + conv_taps[offset]
            * padded[offset : offset + length]
            * tap_valid[:, lag_now : lag_now + 1]
        )
    conv_act = silu_of(conv_out)
    act_low = conv_act.astype(low)
    projected = right_inner(act_low, xproj_t)
    dt_rounded = projected[:, :rank].astype(low)
    b_mat = projected[:, rank : rank + state]
    c_mat = projected[:, rank + state :]
    dt_pre = matmul(dt_rounded, dt_full) + dt_offset
    step_size = jax.nn.softplus(dt_pre)
    drive = step_size * conv_act
    step_far = jnp.where(keep_mask[:, None] > 0, step_size, FAR)
    rate2 = decay_rate * LOG2E
    bx = jnp.broadcast_to(b_mat[:, :, None], (length, state, LANE))
    cx = jnp.broadcast_to(c_mat[:, :, None], (length, state, LANE))
    scanned, starts = scan_forward(step_far, drive, bx, cx, rate2)
    with_skip = scanned + skip_value * conv_act
    gate_act = silu_of(gate_in)
    gated_low = (with_skip * gate_act).astype(low)
    result = inputs_full + matmul(gated_low, out_full)
    output = result.astype(low)
    out_grad = left_inner(gated_low, cotangent)
    gated_grad = right_inner(cotangent, out_full)
    skip_part = gated_grad * gate_act
    gate_grad = gated_grad * with_skip * silu_slope(gate_in)
    gate_low = gate_grad.astype(low)
    gate_in_grad = left_inner(normed_low, gate_low)
    out_share = reduce_grad(out_grad)
    gate_share = reduce_grad(gate_in_grad)
    skip_grad = jnp.sum(skip_part * conv_act, axis=0)
    za, gb, dbx, dcx, rate_grad = scan_backward(step_far, drive, skip_part, bx, cx, rate2, starts)
    a_log_grad = rate_grad * decay_rate
    step_grad = za * LN2 + gb * conv_act
    act_scan = gb * step_size
    b_grad = jnp.sum(dbx, axis=-1)
    c_grad = jnp.sum(dcx, axis=-1)
    pre_grad = step_grad * jax.nn.sigmoid(dt_pre)
    dt_bias_grad = jnp.sum(pre_grad, axis=0)
    pre_low = pre_grad.astype(low)
    dt_weight_grad = left_inner(dt_rounded, pre_low)
    rank_grad = right_inner(pre_low, dt_full)
    proj_grad = jnp.concatenate([rank_grad, b_grad, c_grad], axis=1).astype(low)
    xproj_grad = left_inner(proj_grad, act_low)
    act_grad = matmul(proj_grad, xproj_t) + skip_part * skip_value + act_scan
    conv_grad = act_grad * silu_slope(conv_out)
    conv_bias_grad = jnp.sum(conv_grad, axis=0)
    inner_grad = jnp.zeros_like(inner_in)
    tap_grads = []
    for offset in range(KCONV):
        lag_now = KCONV - 1 - offset
        masked = conv_grad * tap_valid[:, lag_now : lag_now + 1]
        tap_grads.append(jnp.sum(masked * padded[offset : offset + length], axis=0))
        inner_grad = (
            inner_grad + conv_taps[offset] * jnp.pad(masked, ((0, lag_now), (0, 0)))[lag_now:]
        )
    conv_weight_grad = jnp.stack(tap_grads)
    inner_low = inner_grad.astype(low)
    inner_in_grad = left_inner(normed_low, inner_low)
    normed_grad = right_inner(inner_low, in_full[:, :inner_width]) + right_inner(
        gate_low, in_full[:, inner_width:]
    )
    gain_grad = jnp.sum(normed_grad * unit_rows, axis=0)
    scaled = normed_grad * gain_value
    input_grad = cotangent.astype(jnp.float32) + inverse_rms * (
        scaled - unit_rows * jnp.mean(scaled * unit_rows, axis=-1, keepdims=True)
    )
    gain_rows = jnp.pad(gain_grad.reshape(shards, gain_shard), ((0, 0), (0, width - gain_shard)))
    small_grad = jnp.concatenate(
        [
            xproj_grad,
            dt_weight_grad,
            a_log_grad,
            conv_weight_grad,
            conv_bias_grad[None],
            dt_bias_grad[None],
            skip_grad[None],
            gain_rows.reshape(1, -1),
        ],
        axis=0,
    )
    unit = lax.axis_size("dp") * 8
    small_grad = jnp.pad(small_grad, ((0, -small_grad.shape[0] % unit), (0, 0)))
    small_rows = small_grad.shape[0]
    small_grad = jnp.moveaxis(small_grad.reshape(small_rows, shards, width), 1, 0)
    inner_share = reduce_grad(inner_in_grad)
    small_share = reduce_grad(small_grad.reshape(shards * small_rows, width))
    at = xw + rank + state
    return (
        output,
        input_grad,
        small_share[at + KCONV + 3, :gain_shard],
        jnp.concatenate([inner_share, gate_share], axis=1),
        small_share[at : at + KCONV],
        small_share[at + KCONV],
        small_share[:xw].T,
        small_share[xw : xw + rank],
        small_share[at + KCONV + 1],
        small_share[xw + rank : at],
        small_share[at + KCONV + 2],
        out_share,
    )


def reduce_grad(value):
    part = lax.psum_scatter(value.astype(jnp.bfloat16), "fsdp", scatter_dimension=0, tiled=True)
    part = lax.psum_scatter(part, "dp", scatter_dimension=0, tiled=True)
    return lax.all_gather(part, "dp", axis=0, tiled=True).astype(jnp.float32)


def solution(mesh):
    in_specs = (
        P(("dp", "fsdp"), None),
        P(("dp", "fsdp"), None),
        P("fsdp"),
        P("fsdp", None),
        P(None, "fsdp"),
        P("fsdp"),
        P("fsdp", None),
        P(None, "fsdp"),
        P("fsdp"),
        P(None, "fsdp"),
        P("fsdp"),
        P("fsdp", None),
        P(("dp", "fsdp"), None),
    )
    out_specs = (
        P(("dp", "fsdp"), None),
        P(("dp", "fsdp"), None),
        P("fsdp"),
        P("fsdp", None),
        P(None, "fsdp"),
        P("fsdp"),
        P("fsdp", None),
        P(None, "fsdp"),
        P("fsdp"),
        P(None, "fsdp"),
        P("fsdp"),
        P("fsdp", None),
    )
    return jax.shard_map(body, mesh=mesh, in_specs=in_specs, out_specs=out_specs, check_vma=False)
```

time: 1610 us -> 887 us (0.55)
  other arithmetic: 607 us -> 43.4 us
  waiting for transfers between devices: 191 us -> 538 us
  local copies, waits for them, and re-layouts: 371 us -> 30.8 us
  blocking collectives: 323 us -> 41.1 us
  Pallas kernels: 0 us -> 116 us
    psum x1 -> x0, blocking collectives: 262 us -> none  [body(): lax.psum((shares[0], shares[1], shares[2], shares[3], shares[4], shares[5...]
    reduce_scatter x5 -> x8, waiting for transfers between devices: 157 us -> 385 us  [the longest x4 257 us: reduce_grad(): part = lax.psum_scatter(part, 'dp', scatter_dimension=0, tiled=True)]
    reduce_sum x32 -> x2, other arithmetic: 221 us -> 6.79 us  [the longest x1 3.41 us: body(): b_grad = jnp.sum(dbx, axis=-1)]
    mul x37 -> x1, other arithmetic: 188 us -> 0.67 us  [body(): rate2 = decay_rate * LOG2E]
    mul x256 -> x0, local copies, waits for them, and re-layouts: 125 us -> none  [the longest x32 17.2 us: local_step(): carried = factor * carried + b_t[:, :, None] * drive_t[:, None, :]]
    add x49 -> x0, other arithmetic: 122 us -> none  [the longest x16 85.4 us: replay_step(): return (factor * carried + b_t[:, :, None] * drive_t[:, None, :], carried)]
    all_gather x2 -> x5, waiting for transfers between devices: 31.8 us -> 152 us  [the longest x3 86.1 us: reduce_grad(): return lax.all_gather(part, 'dp', axis=0, tiled=True).astype(jnp.float32)]
    pallas_call x0 -> x2, Pallas kernels: none -> 116 us  [the longest x1 84.6 us: scan_backward(): pl.pallas_call(bwd_kernel, grid=(nc, nt), in_specs=[row, row, row, bc, bc...]
  transfers between devices with their start and end apart: 8 -> 13, of which waited for: 6 -> 13; matrix products, arithmetic and copies ran while one was open for 3% -> 8% of each run, Pallas kernels for 0% -> 0%
where the time goes in v1:
time: 887 us; the launch traced here: 876 us
  waiting for transfers between devices  538 us (61%)
  Pallas kernels  116 us (13%)
  matrix products  90.8 us (10%)
  other arithmetic  43.4 us (5%)
  blocking collectives  41.1 us (5%)
  local copies, waits for them, and re-layouts  30.8 us (3%)
  between operations  15.1 us (2%)
    reduce_scatter x4, waiting for transfers between devices, reduce_grad(): part = lax.psum_scatter(part, 'dp', scatter_dimension=0, tiled=True)  257 us
    reduce_scatter x4, waiting for transfers between devices, reduce_grad(): lax.psum_scatter(value.astype(jnp.bfloat16), 'fsdp', scatter_dimension=0,...  127 us
    all_gather x3, waiting for transfers between devices, reduce_grad(): return lax.all_gather(part, 'dp', axis=0, tiled=True).astype(jnp.float32)  86.1 us
    pallas_call x1, Pallas kernels, scan_backward(): pl.pallas_call(bwd_kernel, grid=(nc, nt), in_specs=[row, row, row, bc, bc...  84.6 us
    all_gather x1, waiting for transfers between devices, body(): in_full = lax.all_gather(in_weight, 'fsdp', axis=0, tiled=True)  42.3 us
    dot_general x4, matrix products, matmul(): return jnp.dot(former, latter, preferred_element_type=jnp.float32)  35.7 us
    pallas_call x1, Pallas kernels, scan_forward(): pl.pallas_call(fwd_kernel, grid=(nc, nt), in_specs=[pl.BlockSpec((tc, cg)...  31.7 us
    dot_general x5, matrix products, right_inner(): lax.dot_general(former, latter, (((1,), (1,)), ((), ())), preferred_eleme...  31.7 us
  transfers between devices with their start and end apart: 13, of which 13 were waited for; matrix products, arithmetic and copies ran while one was open for 8% of the time, Pallas kernels for 0%

profile of v1, /device:TPU:0, one launch (start us, length us, event | category | flops | bytes accessed | tf_op | source)
XLA Modules:
  0.0 876.1 jit_solution(11933751279816007798)
XLA Ops:
  7.2 0.7 all-gather.7.cloned.1.call-update
  8.0 0.7 all-gather.9.cloned.1.call-update
  8.7 0.7 broadcast_in_dim.78
  9.4 0.7 broadcast_in_dim.45
  10.1 0.7 broadcast_in_dim.76
  10.8 0.7 broadcast_in_dim.77
  11.4 3.2 concatenate.17
  14.6 10.0 %all-gather = bf16[736,512]{1,0:T(8,128)(2,1)S(1)} all-gather(bf16[184,512]{1,0:T(8,128)(2,1)S(1)} %concatenate.17), channel_id=2, replica_groups=mesh['dp'=8,'fsdp'=4] {'fsdp'}, dimensions={0}, use_global_device_ids=true | all-gather | bytes 942080 | tf_op jit(solution)/shard_map/all_gather | solution.py:300
  25.3 0.8 copy.50
  26.3 0.6 copy.54
  27.6 0.7 broadcast_multiply_fusion.3.a_ref
  28.3 42.3 %all-gather.7.cloned.1.call-done = bf16[1024,4096]{1,0:T(8,128)(2,1)} async-done(((bf16[256,4096]{1,0:T(8,128)(2,1)}), bf16[1024,4096]{1,0:T(8,128)(2,1)}) %all-gather.7.cloned.1.call-update) | async-done | bytes 8388624 | tf_op jit(solution)/shard_map/all_gather | solution.py:299
  70.6 7.1 fusion.41
  77.7 3.8 copy-done
  81.5 2.5 slice.183
  84.0 23.2 %all-gather.9.cloned.1.call-done = bf16[2048,1024]{1,0:T(8,128)(2,1)} async-done(((bf16[512,1024]{1,0:T(8,128)(2,1)}), bf16[2048,1024]{1,0:T(8,128)(2,1)}) %all-gather.9.cloned.1.call-update) | async-done | bytes 4194320 | tf_op jit(solution)/shard_map/all_gather | solution.py:301
  107.3 16.6 %multiply_reduce_fusion = (bf16[2048]{0:T(1024)(128)(2,1)}, f32[512,2048]{1,0:T(8,128)}, f32[512,2048]{1,0:T(8,128)S(1)}, f32[512,2048]{1,0:T(8,128)}) fusion(f32[512,4096]{1,0:T(8,128)} %copy-done, f32[512]{0:T(512)S(1)} %bitcast.106, f32[512,2048]{1,0:T(8,128)} %slice.183, f32[2048]{0:T(1024)S(1)} %bitcast.93, f32[512]{0:T(512)S(1)} %bitcast.114, ...), kind=kOutput, calls=%fused_computation.15 | convolution fusion | flops 2171598848 | bytes 26267648 | tf_op jit(solution)/shard_map/dot_general | solution.py:30
  123.9 1.3 fusion.31
  125.2 0.7 copy-done.1
  126.2 7.9 fusion.38
  134.2 2.6 broadcast_in_dim.80.b_ref
  136.7 2.6 broadcast_in_dim.81.c_ref
  139.3 31.7 %scan_forward.1 = (f32[512,2048]{1,0:T(8,128)}, f32[16,16,2048]{2,1,0:T(8,128)}) custom-call(f32[512,2048]{1,0:T(8,128)} %get-tuple-element.46.dt_ref, f32[512,2048]{1,0:T(8,128)} %get-tuple-element.45.dr_ref, f32[512,16,128]{2,1,0:T(8,128)} %broadcast_in_dim.80.b_ref, f32[512,16,128]{2,1,0:T(8,128)} %broadcast_in_dim.81.c_ref, ...), custom_call_target="tpu_custom_call" | custom-call | tf_op jit(solution)/shard_map/scan_forward/pallas_call | solution.py:121
  171.0 84.6 %scan_backward.1 = (f32[512,2048]{1,0:T(8,128)}, f32[512,2048]{1,0:T(8,128)}, f32[512,16,128]{2,1,0:T(8,128)}, f32[512,16,128]{2,1,0:T(8,128)}, f32[16,2048]{1,0:T(8,128)}) custom-call(f32[512,2048]{1,0:T(8,128)} %get-tuple-element.46.dt_ref, f32[512,2048]{1,0:T(8,128)} %get-tuple-element.45.dr_ref, f32[512,2048]{1,0:T(8,128)} %get-tuple-element.34.dy_ref, ...), custom_call_target="tpu_custom_call" | custom-call | tf_op jit(solution)/shard_map/scan_backward/pallas_call | solution.py:248
  255.6 6.7 fusion.47
  262.3 1.4 convolution_convert_fusion.5
  263.7 3.4 reduce_sum.109
  267.2 3.4 reduce_sum.110
  270.7 17.3 %multiply_reduce_fusion.2 = (bf16[2048]{0:T(1024)(128)(2,1)S(1)}, bf16[2048]{0:T(1024)(128)(2,1)S(1)}, bf16[2048]{0:T(1024)(128)(2,1)S(1)}, f32[512,2048]{1,0:T(...) fusion(f32[512,2048]{1,0:T(8,128)} %slice.183, f32[512]{0:T(512)} %bitcast.115, ...), kind=kOutput, calls=%fused_computation.17 | convolution fusion | flops 230975488 | bytes 38275072 | tf_op jit(solution)/shard_map/dot_general | solution.py:20
  288.1 16.8 %fusion.45 = (bf16[2048]{0:T(1024)(128)(2,1)S(1)}, bf16[2048]{0:T(1024)(128)(2,1)S(1)}, bf16[512,2048]{1,0:T(8,128)(2,1)}, bf16[512,2048]{1,0:T(8,128)(2,1)}, bf16[512,2048]{1,0:T(8,128)(2,1)}) fusion(f32[512,2048]{1,0:T(8,128)} %get-tuple-element.66, f32[512,4096]{1,0:T(8,128)} %copy-done, f32[512]{0:T(512)S(1)} %bitcast.107, ...), kind=kLoop, calls=%fused_computation.96 | loop fusion | flops 32501760 | bytes 44091392 | tf_op jit(solution)/shard_map/reduce_sum | solution.py:381
  305.0 6.0 convolution_convert_fusion
  311.6 6.1 convolution_convert_fusion.2
  317.8 6.4 convolution_convert_fusion.1
  324.5 5.3 fusion.7
  329.8 7.0 fusion.22
  336.9 0.6 stack.19
  337.5 0.6 stack.16
  338.1 0.6 stack.17
  339.3 0.6 broadcast_in_dim.83
  339.9 0.6 broadcast_in_dim.84
  340.5 1.4 convolution_convert_fusion.4
  341.9 0.9 multiply_convert_fusion.2
  342.9 3.7 convolution_convert_fusion.3
  347.7 1.0 copy.44
  348.8 6.9 reduce-scatter.21.cloned.1.call-done
  355.8 46.9 %reduce-scatter.13.cloned.1.call-done = bf16[256,2048]{1,0:T(8,128)(2,1)} async-done(((bf16[1024,2048]{1,0:T(8,128)(2,1)}), bf16[256,2048]{1,0:T(8,128)(2,1)}) %reduce-scatter.13.cloned.1.call-update) | async-done | bytes 1048592 | tf_op jit(solution)/shard_map/reduce_scatter | solution.py:440
  402.8 47.5 %reduce-scatter.17.cloned.1.call-done = bf16[256,2048]{1,0:T(8,128)(2,1)} async-done(((bf16[1024,2048]{1,0:T(8,128)(2,1)}), bf16[256,2048]{1,0:T(8,128)(2,1)}) %reduce-scatter.17.cloned.1.call-update) | async-done | bytes 1048592 | tf_op jit(solution)/shard_map/reduce_scatter | solution.py:440
  450.3 26.1 %reduce-scatter.9.cloned.1.call-done = bf16[192,512]{1,0:T(8,128)(2,1)} async-done(((bf16[768,512]{1,0:T(8,128)(2,1)}), bf16[192,512]{1,0:T(8,128)(2,1)}) %reduce-scatter.9.cloned.1.call-update) | async-done | bytes 196624 | tf_op jit(solution)/shard_map/reduce_scatter | solution.py:440
  476.5 67.5 %reduce-scatter.23.cloned.1.call-done = bf16[64,1024]{1,0:T(8,128)(2,1)} async-done(((bf16[512,1024]{1,0:T(8,128)(2,1)}), bf16[64,1024]{1,0:T(8,128)(2,1)}) %reduce-scatter.23.cloned.1.call-update) | async-done | bytes 131088 | tf_op jit(solution)/shard_map/reduce_scatter | solution.py:441
  544.1 66.5 %reduce-scatter.15.cloned.1.call-done = bf16[32,2048]{1,0:T(8,128)(2,1)} async-done(((bf16[256,2048]{1,0:T(8,128)(2,1)}), bf16[32,2048]{1,0:T(8,128)(2,1)}) %reduce-scatter.15.cloned.1.call-update) | async-done | bytes 131088 | tf_op jit(solution)/shard_map/reduce_scatter | solution.py:441
  610.7 66.5 %reduce-scatter.19.cloned.1.call-done = bf16[32,2048]{1,0:T(8,128)(2,1)} async-done(((bf16[256,2048]{1,0:T(8,128)(2,1)}), bf16[32,2048]{1,0:T(8,128)(2,1)}) %reduce-scatter.19.cloned.1.call-update) | async-done | bytes 131088 | tf_op jit(solution)/shard_map/reduce_scatter | solution.py:441
  677.2 4.0 fusion.21
  681.2 3.4 fusion.24
  684.6 56.6 %reduce-scatter.11.cloned.1.call-done = bf16[24,512]{1,0:T(8,128)(2,1)} async-done(((bf16[192,512]{1,0:T(8,128)(2,1)}), bf16[24,512]{1,0:T(8,128)(2,1)}) %reduce-scatter.11.cloned.1.call-update) | async-done | bytes 24592 | tf_op jit(solution)/shard_map/reduce_scatter | solution.py:441
  741.2 31.2 %all_gather.28 = bf16[192,512]{1,0:T(8,128)(2,1)S(1)} all-gather(bf16[24,512]{1,0:T(8,128)(2,1)} %reduce-scatter.11.cloned.1.call-done), channel_id=1, replica_groups=mesh['dp'=8,'fsdp'=4] {'dp'}, dimensions={0}, use_global_device_ids=true | all-gather | bytes 221184 | tf_op jit(solution)/shard_map/all_gather | solution.py:442
  772.5 0.7 slice.206
  773.1 0.6 slice.208
  773.7 0.6 slice.203
  775.5 0.7 slice_bitcast_fusion
  776.2 6.3 all-gather.15.cloned.1.call-done
  782.5 2.8 convert_element_type.162
  785.3 38.7 %all-gather.11.cloned.1.call-done = bf16[256,2048]{1,0:T(8,128)(2,1)} async-done(((bf16[32,2048]{1,0:T(8,128)(2,1)}), bf16[256,2048]{1,0:T(8,128)(2,1)}) %all-gather.11.cloned.1.call-update) | async-done | bytes 1048592 | tf_op jit(solution)/shard_map/all_gather | solution.py:442
  824.0 41.1 %all-gather.13.cloned.1.call-done = bf16[256,2048]{1,0:T(8,128)(2,1)} async-done(((bf16[32,2048]{1,0:T(8,128)(2,1)}), bf16[256,2048]{1,0:T(8,128)(2,1)}) %all-gather.13.cloned.1.call-update) | async-done | bytes 1048592 | tf_op jit(solution)/shard_map/all_gather | solution.py:442
  865.1 4.0 maximum_convert_fusion
  (152 shorter events, 6.3 us)
Async XLA Ops:
  7.2 19.8 %copy-start.43 = (s32[1,8]{1,0:T(1,128)S(1)}, s32[1,8]{1,0:T(1,128)}, u32[]{:S(2)}) copy-start(s32[1,8]{1,0:T(1,128)} %param.14) | copy-start | bytes 100
  7.2 20.0 %copy-start.4 = (bf16[512,1024]{1,0:T(8,128)(2,1)S(1)}, bf16[512,1024]{1,0:T(8,128)(2,1)}, u32[]{:S(2)}) copy-start(bf16[512,1024]{1,0:T(8,128)(2,1)} %param.13) | copy-start | bytes 3145732
  7.2 63.4 %all-gather.7.cloned.1.call-start = ((), (), s32[]{:S(2)}) async-start(), calls=%async_computation.8 | async-start | bytes 10485760 | tf_op jit(solution)/shard_map/all_gather | solution.py:299
  7.9 99.3 %all-gather.9.cloned.1.call-start = ((), (), s32[]{:S(2)}) async-start(), calls=%async_computation.9 | async-start | bytes 5242880 | tf_op jit(solution)/shard_map/all_gather | solution.py:301
  8.7 347.0 %reduce-scatter.21.cloned.1.call-start = ((), (), s32[]{:S(2)}) async-start(), calls=%async_computation.18 | async-start | bytes 5242880 | tf_op jit(solution)/shard_map/reduce_scatter | solution.py:440
  25.3 82.0 %copy-start.12 = (f32[1,4,4,128]{3,1,2,0:T(4,128)}, f32[1,4,4,128]{3,1,2,0:T(4,128)S(1)}, u32[]{:S(2)}) copy-start(f32[1,4,4,128]{3,1,2,0:T(4,128)S(1)} %copy.48) | copy-start | bytes 24580
  25.3 81.9 %copy-start.14 = (f32[1,4,4,128]{3,1,2,0:T(4,128)}, f32[1,4,4,128]{3,1,2,0:T(4,128)S(1)}, u32[]{:S(2)}) copy-start(f32[1,4,4,128]{3,1,2,0:T(4,128)S(1)} %copy.49) | copy-start | bytes 24580
  26.2 100.1 %copy-start.17 = (f32[1,4,4,128]{3,1,2,0:T(4,128)}, f32[1,4,4,128]{3,1,2,0:T(4,128)S(1)}, u32[]{:S(2)}) copy-start(f32[1,4,4,128]{3,1,2,0:T(4,128)S(1)} %copy.52) | copy-start | bytes 24580
  27.5 50.2 %copy-start.32 = (f32[512]{0:T(512)}, f32[512]{0:T(512)S(1)}, u32[]{:S(2)}) copy-start(f32[512]{0:T(512)S(1)} %add_rsqrt_fusion) | copy-start | bytes 6148
  27.6 79.7 %copy-start.35 = (f32[512,1]{0,1:T(1,128)}, f32[512,1]{0,1:T(1,128)S(1)}, u32[]{:S(2)}) copy-start(f32[512,1]{0,1:T(1,128)S(1)} %get-tuple-element.61) | copy-start | bytes 6148
  27.6 79.7 %copy-start.39 = (f32[512,1]{0,1:T(1,128)}, f32[512,1]{0,1:T(1,128)S(1)}, u32[]{:S(2)}) copy-start(f32[512,1]{0,1:T(1,128)S(1)} %get-tuple-element.60) | copy-start | bytes 6148
  27.6 79.7 %copy-start.40 = (f32[512,1]{0,1:T(1,128)}, f32[512,1]{0,1:T(1,128)S(1)}, u32[]{:S(2)}) copy-start(f32[512,1]{0,1:T(1,128)S(1)} %get-tuple-element.62) | copy-start | bytes 6148
  27.6 79.7 %copy-start.41 = (f32[512,1]{0,1:T(1,128)}, f32[512,1]{0,1:T(1,128)S(1)}, u32[]{:S(2)}) copy-start(f32[512,1]{0,1:T(1,128)S(1)} %get-tuple-element.63) | copy-start | bytes 6148
  27.6 50.1 %copy-start.27 = (f32[4,1,256]{2,1,0:T(1,128)}, f32[4,1,256]{2,1,0:T(1,128)S(1)}, u32[]{:S(2)}) copy-start(f32[4,1,256]{2,1,0:T(1,128)S(1)} %slice_convert_fusion.4) | copy-start | bytes 12292
  77.7 3.8 copy-start
  81.5 25.8 %copy-start.7 = (bf16[512,1024]{1,0:T(8,128)(2,1)S(1)}, bf16[512,1024]{1,0:T(8,128)(2,1)}, u32[]{:S(2)}) copy-start(bf16[512,1024]{1,0:T(8,128)(2,1)} %param.25) | copy-start | bytes 3145732
  107.3 16.6 %copy-start.9 = (bf16[12,8,4,512]{3,1,2,0:T(8,128)(2,1)S(1)}, bf16[12,8,4,512]{3,1,2,0:T(8,128)(2,1)}, u32[]{:S(2)}) copy-start(bf16[12,8,4,512]{3,1,2,0:T(8,128)(2,1)} %copy.50) | copy-start | bytes 1179652
  123.9 2.0 copy-start.1
  126.0 8.2 copy-start.10
  171.0 84.6 %copy-start.2 = (f32[512,2048]{1,0:T(8,128)S(1)}, f32[512,2048]{1,0:T(8,128)}, u32[]{:S(2)}) copy-start(f32[512,2048]{1,0:T(8,128)} %copy-done.1) | copy-start | bytes 12582916
  171.0 84.6 %copy-start.18 = (f32[1,4,4,128]{3,1,2,0:T(4,128)S(1)}, f32[1,4,4,128]{3,1,2,0:T(4,128)}, u32[]{:S(2)}) copy-start(f32[1,4,4,128]{3,1,2,0:T(4,128)} %copy-done.17) | copy-start | bytes 24580
  263.7 7.0 copy-start.11
  263.7 7.0 copy-start.16
  263.7 7.0 copy-start.19
  267.2 20.9 %copy-start.30 = (bf16[512,16]{0,1:T(8,128)(2,1)}, bf16[512,16]{0,1:T(8,128)(2,1)S(1)}, u32[]{:S(2)}) copy-start(bf16[512,16]{0,1:T(8,128)(2,1)S(1)} %copy.42) | copy-start | bytes 49156
  270.6 17.4 %copy-start.31 = (bf16[512,16]{0,1:T(8,128)(2,1)}, bf16[512,16]{0,1:T(8,128)(2,1)S(1)}, u32[]{:S(2)}) copy-start(bf16[512,16]{0,1:T(8,128)(2,1)S(1)} %copy.43) | copy-start | bytes 49156
  270.7 17.4 %copy-start.3 = (f32[512,2048]{1,0:T(8,128)S(1)}, f32[512,2048]{1,0:T(8,128)}, u32[]{:S(2)}) copy-start(f32[512,2048]{1,0:T(8,128)} %copy-done.1) | copy-start | bytes 12582916
  270.7 17.4 %copy-start.13 = (f32[1,4,4,128]{3,1,2,0:T(4,128)S(1)}, f32[1,4,4,128]{3,1,2,0:T(4,128)}, u32[]{:S(2)}) copy-start(f32[1,4,4,128]{3,1,2,0:T(4,128)} %copy-done.12) | copy-start | bytes 24580
  270.7 17.4 %copy-start.15 = (f32[1,4,4,128]{3,1,2,0:T(4,128)S(1)}, f32[1,4,4,128]{3,1,2,0:T(4,128)}, u32[]{:S(2)}) copy-start(f32[1,4,4,128]{3,1,2,0:T(4,128)} %copy-done.14) | copy-start | bytes 24580
  270.7 17.4 %copy-start.36 = (f32[512,1]{0,1:T(1,128)S(1)}, f32[512,1]{0,1:T(1,128)}, u32[]{:S(2)}) copy-start(f32[512,1]{0,1:T(1,128)} %copy-done.35) | copy-start | bytes 6148
  288.1 16.9 %copy-start.8 = (bf16[512,1024]{1,0:T(8,128)(2,1)S(1)}, bf16[512,1024]{1,0:T(8,128)(2,1)}, u32[]{:S(2)}) copy-start(bf16[512,1024]{1,0:T(8,128)(2,1)} %param.25) | copy-start | bytes 3145732
  310.9 0.7 copy-start.28
  310.9 0.7 copy-start.33
  311.0 91.7 %reduce-scatter.13.cloned.1.call-start = ((), (), s32[]{:S(2)}) async-start(), calls=%async_computation.12 | async-start | bytes 5242880 | tf_op jit(solution)/shard_map/reduce_scatter | solution.py:440
  317.7 132.5 %reduce-scatter.17.cloned.1.call-start = ((), (), s32[]{:S(2)}) async-start(), calls=%async_computation.15 | async-start | bytes 5242880 | tf_op jit(solution)/shard_map/reduce_scatter | solution.py:440
  324.2 152.3 %reduce-scatter.9.cloned.1.call-start = ((), (), s32[]{:S(2)}) async-start(), calls=%async_computation.10 | async-start | bytes 983040 | tf_op jit(solution)/shard_map/reduce_scatter | solution.py:440
  324.5 5.3 copy-start.6
  329.8 9.5 %copy-start.26 = (bf16[2048]{0:T(1024)(128)(2,1)S(1)}, bf16[2048]{0:T(1024)(128)(2,1)}, u32[]{:S(2)}) copy-start(bf16[2048]{0:T(1024)(128)(2,1)} %get-tuple-element.36) | copy-start | bytes 12292
  329.8 10.1 %copy-start.37 = (bf16[2048]{0:T(1024)(128)(2,1)S(1)}, bf16[2048]{0:T(1024)(128)(2,1)}, u32[]{:S(2)}) copy-start(bf16[2048]{0:T(1024)(128)(2,1)} %get-tuple-element.33) | copy-start | bytes 12292
  342.8 3.8 copy-start.20
  342.9 3.8 copy-start.21
  342.9 3.7 copy-start.22
  342.9 3.7 copy-start.23
  342.9 3.7 copy-start.24
  342.9 3.7 copy-start.25
  347.1 330.1 %copy-start.38 = (f32[512]{0:T(512)S(1)}, f32[512]{0:T(512)}, u32[]{:S(2)}) copy-start(f32[512]{0:T(512)} %get-tuple-element.32) | copy-start | bytes 6148
  347.1 330.2 %copy-start.29 = (f32[4,1,256]{2,1,0:T(1,128)S(1)}, f32[4,1,256]{2,1,0:T(1,128)}, u32[]{:S(2)}) copy-start(f32[4,1,256]{2,1,0:T(1,128)} %copy-done.27) | copy-start | bytes 12292
  347.1 330.2 %copy-start.34 = (f32[512]{0:T(512)S(1)}, f32[512]{0:T(512)}, u32[]{:S(2)}) copy-start(f32[512]{0:T(512)} %copy-done.32) | copy-start | bytes 6148
  348.7 195.3 %reduce-scatter.23.cloned.1.call-start = ((), (), s32[]{:S(2)}) async-start(), calls=%async_computation.19 | async-start | bytes 1179648 | tf_op jit(solution)/shard_map/reduce_scatter | solution.py:441
  355.7 254.9 %reduce-scatter.15.cloned.1.call-start = ((), (), s32[]{:S(2)}) async-start(), calls=%async_computation.13 | async-start | bytes 1179648 | tf_op jit(solution)/shard_map/reduce_scatter | solution.py:441
  402.7 278.5 %copy-start.5 = (bf16[512,2048]{1,0:T(8,128)(2,1)S(1)}, bf16[512,2048]{1,0:T(8,128)(2,1)}, u32[]{:S(2)}) copy-start(bf16[512,2048]{1,0:T(8,128)(2,1)} %get-tuple-element.43) | copy-start | bytes 6291460
  402.7 274.5 %reduce-scatter.19.cloned.1.call-start = ((), (), s32[]{:S(2)}) async-start(), calls=%async_computation.16 | async-start | bytes 1179648 | tf_op jit(solution)/shard_map/reduce_scatter | solution.py:441
  450.3 291.0 %reduce-scatter.11.cloned.1.call-start = ((), (), s32[]{:S(2)}) async-start(), calls=%async_computation.11 | async-start | bytes 221184 | tf_op jit(solution)/shard_map/reduce_scatter | solution.py:441
  476.5 306.0 %all-gather.15.cloned.1.call-start = ((), (), s32[]{:S(2)}) async-start(), calls=%async_computation.20 | async-start | bytes 1179648 | tf_op jit(solution)/shard_map/all_gather | solution.py:442
  544.1 279.9 %all-gather.11.cloned.1.call-start = ((), (), s32[]{:S(2)}) async-start(), calls=%async_computation.14 | async-start | bytes 1179648 | tf_op jit(solution)/shard_map/all_gather | solution.py:442
  610.6 254.5 %all-gather.13.cloned.1.call-start = ((), (), s32[]{:S(2)}) async-start(), calls=%async_computation.17 | async-start | bytes 1179648 | tf_op jit(solution)/shard_map/all_gather | solution.py:442
  677.2 4.0 copy-start.42
Sparse Core Ops, SparseCore 0:
  9.6 60.9 all-gather.6
  72.1 35.0 all-gather.8
  311.1 44.5 reduce-scatter.20
  358.1 44.5 reduce-scatter.12
  405.6 44.5 reduce-scatter.16
  453.2 23.1 reduce-scatter.8
  479.8 64.1 reduce-scatter.22
  547.4 63.1 reduce-scatter.14
  614.0 63.1 reduce-scatter.18
  680.3 60.9 reduce-scatter.10
  743.4 39.0 all-gather.14
  784.5 39.4 all-gather.10
  826.1 38.9 all-gather.12
